TPU v7x, 32 devices: a whole 2x2x4 slice. The times are simulated.
32 devices in a mesh: seq: 2 (over x), tensor: 4 (over z), bucket: 4 (over y, core).
Axes of the slice: x: 2, y: 2, z: 4, core: 2. Of those that a mesh axis runs over, the one named last changes fastest.
Arguments:
- queries: bfloat16 [4, 1024, 3072], P('bucket', ('seq', 'tensor')), may hold values from -6 to 6
- keys: bfloat16 [4, 1024, 3072], P('bucket', ('seq', 'tensor')), may hold values from -6 to 6
- values: bfloat16 [4, 1024, 3072], P('bucket', ('seq', 'tensor')), may hold values from -6 to 6
- lengths: int32 [4], P('bucket'), may hold values from 256 to 1024, as said below
- out_weight: bfloat16 [3072, 3072], P(('seq', 'bucket'), 'tensor'), may hold values from -0.109375 to 0.109375
Outputs:
- projected: bfloat16 [4, 1024, 3072], P('bucket', ('seq', 'tensor'))
Inputs may be any that keep to these rules, and one draw needn't show every extreme that they name: `lengths`: each bucket has 256 to 1024 live tokens, and at least one bucket has all 1024.
All inputs are finite; a program needn't handle non-finite values.
Results may differ from a plain program's by a relative error of at most 0.018.
Values may be sent and summed in bfloat16 or wider, within the bound.
No kernel may reach another device: no remote copies, remote signals or barrier semaphores. Data moves between devices by JAX's collectives and lax.ppermute only.
A program may use at most 128 MiB of HBM per device.

v0:
```python
import jax
import jax.numpy as jnp
from jax import lax
from jax.sharding import PartitionSpec as P

HS = 128
MASKED_SCORE = -1e30


def shards(queries, keys, values, lengths, out_weight):
    tok_rows = queries.shape[1]
    n_tensor = lax.axis_size("tensor")
    tensor_index = lax.axis_index("tensor")
    live_len = lengths[0]
    local_q, local_k, local_v = (
        lax.all_to_all(queries[0], "seq", split_axis=1, concat_axis=0, tiled=True),
        lax.all_to_all(keys[0], "seq", split_axis=1, concat_axis=0, tiled=True),
        lax.all_to_all(values[0], "seq", split_axis=1, concat_axis=0, tiled=True),
    )
    row_count, col_count = local_q.shape
    head_count = col_count // HS
    query_heads = local_q.reshape(row_count, head_count, HS)

    def spots(first_row, total_rows):
        index_row = first_row + jnp.arange(total_rows, dtype=jnp.int32)
        owner = index_row // row_count
        within = index_row % row_count
        return (within // tok_rows * n_tensor + owner) * tok_rows + within % tok_rows

    query_usable = spots(tensor_index * row_count, row_count) < live_len
    initial = (
        jnp.full((row_count, head_count), MASKED_SCORE, jnp.float32),
        jnp.zeros((row_count, head_count), jnp.float32),
        jnp.zeros((row_count, head_count, HS), jnp.float32),
    )
    carried = initial
    first_row = jnp.int32(0)
    key_rows = lax.all_gather(local_k, "tensor", axis=0, tiled=True)
    value_rows = lax.all_gather(local_v, "tensor", axis=0, tiled=True)
    for offset in range(key_rows.shape[0] // row_count):
        row_peak, row_sum, accumulated = carried
        key_tile = key_rows[offset * row_count : (offset + 1) * row_count].reshape(
            row_count, head_count, HS
        )
        value_tile = value_rows[offset * row_count : (offset + 1) * row_count].reshape(
            row_count, head_count, HS
        )
        key_usable = spots(first_row + offset * row_count, row_count) < live_len
        scores = jnp.einsum(
            "qhd,khd->qhk", query_heads, key_tile, preferred_element_type=jnp.float32
        ) * HS ** (-0.5)
        scores = jnp.where(key_usable[None, None, :], scores, MASKED_SCORE)
        peak_new = jnp.maximum(row_peak, jnp.max(scores, axis=-1))
        exponent = jnp.where(key_usable[None, None, :], jnp.exp(scores - peak_new[..., None]), 0.0)
        rescale = jnp.exp(row_peak - peak_new)
        accumulated = accumulated * rescale[..., None] + jnp.einsum(
            "qhk,khd->qhd",
            exponent.astype(jnp.bfloat16),
            value_tile,
            preferred_element_type=jnp.float32,
        )
        carried = (peak_new, row_sum * rescale + jnp.sum(exponent, axis=-1), accumulated)
    row_peak, row_sum, accumulated = carried
    attended = accumulated / row_sum[..., None]
    mixed = jnp.where(query_usable[:, None], attended.reshape(row_count, col_count), 0.0).astype(
        jnp.bfloat16
    )
    restored = lax.all_to_all(mixed, "seq", split_axis=0, concat_axis=1, tiled=True)
    wide_weight = lax.all_gather(out_weight, "tensor", axis=1, tiled=True)
    summed = jnp.dot(
        restored,
        lax.all_gather(wide_weight, ("seq", "bucket"), axis=0, tiled=True),
        preferred_element_type=jnp.float32,
    )
    return summed.astype(jnp.bfloat16)[None]


def solution(mesh):
    in_specs = (
        P("bucket", ("seq", "tensor"), None),
        P("bucket", ("seq", "tensor"), None),
        P("bucket", ("seq", "tensor"), None),
        P("bucket"),
        P(("seq", "bucket"), "tensor"),
    )
    out_specs = P("bucket", ("seq", "tensor"), None)
    return jax.shard_map(shards, mesh=mesh, in_specs=in_specs, out_specs=out_specs, check_vma=False)
```

profile of v0, /device:TPU:0, one launch (start us, length us, event | category | flops | bytes accessed | tf_op | source)
XLA Modules:
  0.0 309.9 jit_solution(5005568359367810147)
XLA Ops:
  6.5 0.0 copy-start
  6.5 0.0 all-gather.9.cloned.1.call-start
  6.5 0.7 all-gather.9.cloned.1.call-update
  7.3 0.0 all-gather.5.cloned.1.call-start
  7.3 1.5 copy.68
  8.8 14.8 %all_to_all.70 = bf16[128,2,1536]{0,2,1:T(8,128)(2,1)S(1)} all-to-all(bf16[128,2,1536]{0,2,1:T(8,128)(2,1)S(1)} %bitcast.125), channel_id=1, replica_groups=mesh['seq'=2,'tensor'=4,'bucket'=4] {'seq'}, dimensions={1} | all-to-all | bytes 1572864 | tf_op jit(solution)/shard_map/all_to_all | solution.py:17
  23.6 1.2 copy.69
  24.8 0.0 all-gather.5.cloned.1.call-update
  24.8 0.0 all-gather.7.cloned.1.call-start
  24.9 0.0 copy-done
  24.9 0.4 copy.75
  25.3 0.0 copy-start.1
  25.3 12.5 %all_to_all.71 = bf16[128,2,1536]{0,2,1:T(8,128)(2,1)S(1)} all-to-all(bf16[128,2,1536]{0,2,1:T(8,128)(2,1)S(1)} %bitcast.126), channel_id=1, replica_groups=mesh['seq'=2,'tensor'=4,'bucket'=4] {'seq'}, dimensions={1} | all-to-all | bytes 1572864 | tf_op jit(solution)/shard_map/all_to_all | solution.py:18
  37.8 1.2 copy.76
  38.9 0.0 all-gather.7.cloned.1.call-update
  39.0 0.0 all-gather.11.cloned.1.call-start
  39.0 22.6 %all-gather.9.cloned.1.call-done = bf16[384,3072]{1,0:T(8,128)(2,1)} async-done(((bf16[384,768]{1,0:T(8,128)(2,1)}), bf16[384,3072]{1,0:T(8,128)(2,1)}) %all-gather.9.cloned.1.call-update) | async-done | bytes 2359312 | tf_op jit(solution)/shard_map/all_gather | solution.py:69
  61.6 0.0 all-gather.11.cloned.1.call-update
  61.7 0.0 copy-done.1
  61.7 1.2 copy.71
  62.8 3.5 %all-to-all-start.1 = ((bf16[128,2,1536]{0,2,1:T(8,128)(2,1)}), bf16[128,2,1536]{0,2,1:T(8,128)(2,1)S(1)}, u32[]{:S(2)}, u32[]{:S(2)}) async-start(bf16[128,2,1536]{0,2,1:T(8,128)(2,1)} %bitcast.5), calls=%async_computation.1 | async-start | bytes 1572864 | tf_op jit(solution)/shard_map/all_to_all | solution.py:16
  67.1 10.2 %all-to-all-done.1 = bf16[128,2,1536]{0,2,1:T(8,128)(2,1)S(1)} async-done(((bf16[128,2,1536]{0,2,1:T(8,128)(2,1)}), bf16[128,2,1536]{0,2,1:T(8,128)(2,1)S(1)}, u32[]{:S(2)}, u32[]{:S(2)}) %all-to-all-start.1) | async-done | bytes 786464 | tf_op jit(solution)/shard_map/all_to_all | solution.py:16
  77.3 6.7 %copy.72 = bf16[2,128,1536]{1,0,2:T(2,128)(2,1)S(1)} copy(bf16[2,128,1536]{1,2,0:T(8,128)(2,1)S(1)} %bitcast.122) | data formatting | bytes 1572864 | tf_op jit(solution)/shard_map/all_to_all | solution.py:16
  83.9 0.5 reshape.424
  84.4 41.0 %all-gather.5.cloned.1.call-done = bf16[1024,1536]{1,0:T(8,128)(2,1)} async-done(((bf16[256,1536]{1,0:T(8,128)(2,1)}), bf16[1024,1536]{1,0:T(8,128)(2,1)}) %all-gather.5.cloned.1.call-update) | async-done | bytes 3145744 | tf_op jit(solution)/shard_map/all_gather | solution.py:38
  125.4 2.9 fusion.89
  128.4 1.2 copy.70
  129.6 0.3 copy.92
  129.8 0.3 copy.86
  130.1 1.4 copy.80
  131.5 57.6 %all-gather.7.cloned.1.call-done = bf16[1024,1536]{1,0:T(8,128)(2,1)} async-done(((bf16[256,1536]{1,0:T(8,128)(2,1)}), bf16[1024,1536]{1,0:T(8,128)(2,1)}) %all-gather.7.cloned.1.call-update) | async-done | bytes 3145744 | tf_op jit(solution)/shard_map/all_gather | solution.py:39
  189.1 3.6 %fusion.88 = (bf16[256,1536]{1,0:T(8,128)(2,1)}, bf16[256,1536]{1,0:T(8,128)(2,1)}, bf16[256,1536]{1,0:T(8,128)(2,1)}, bf16[256,1536]{1,0:T(8,128)(2,1)}) fusion(bf16[1024,1536]{1,0:T(8,128)(2,1)} %all-gather.7.cloned.1.call-done), kind=kLoop, calls=%fused_computation.155 | loop fusion | bytes 6291456 | tf_op jit(solution)/shard_map/slice | solution.py:45
  192.7 2.3 copy.83
  195.0 2.5 copy.89
  197.5 2.4 copy.95
  199.9 2.5 copy.77
  202.4 1.9 bitcast_reduce_fusion.3
  204.3 0.8 bitcast_reduce_fusion
  205.2 0.8 bitcast_reduce_fusion.1
  206.1 0.8 bitcast_reduce_fusion.2
  206.9 0.8 fusion.11
  207.8 0.8 fusion.13
  208.6 0.0 copy-start.5
  208.6 0.8 fusion.15
  209.5 0.8 fusion.9
  210.4 0.0 copy-done.5
  210.4 0.0 copy-start.4
  210.4 1.2 fusion.21
  211.5 0.0 copy-done.4
  211.6 0.0 copy-start.3
  211.6 1.4 fusion.19
  212.9 0.0 copy-done.3
  212.9 0.0 copy-start.2
  212.9 1.2 fusion.17
  214.2 0.0 copy-done.2
  214.2 3.0 fusion.25
  217.2 0.3 copy.98
  217.5 0.2 reshape.432
  217.7 0.8 select_convert_fusion
  218.4 0.1 copy.99
  218.6 16.7 %all_to_all.72 = bf16[2,128,1536]{1,2,0:T(8,128)(2,1)S(1)} all-to-all(bf16[2,128,1536]{1,2,0:T(8,128)(2,1)S(1)} %copy.99), channel_id=1, replica_groups=mesh['seq'=2,'tensor'=4,'bucket'=4] {'seq'}, dimensions={0} | all-to-all | bytes 1572864 | tf_op jit(solution)/shard_map/all_to_all | solution.py:68
  235.3 58.3 %all-gather.11.cloned.1.call-done = bf16[3072,3072]{1,0:T(8,128)(2,1)} async-done(((bf16[384,3072]{1,0:T(8,128)(2,1)}), bf16[3072,3072]{1,0:T(8,128)(2,1)}) %all-gather.11.cloned.1.call-update) | async-done | bytes 18874384 | tf_op jit(solution)/shard_map/all_gather | solution.py:72
  293.5 9.9 %fusion = bf16[1,128,3072]{2,1,0:T(8,128)(2,1)} fusion(bf16[128,3072]{0,1:T(8,128)(2,1)S(1)} %bitcast.115, bf16[3072,3072]{1,0:T(8,128)(2,1)} %all-gather.11.cloned.1.call-done), kind=kOutput, calls=%fused_computation.1 | convolution fusion | flops 2416312320 | bytes 20447232 | tf_op jit(solution)/shard_map/dot_general | solution.py:70
  (5 shorter events, 0.1 us)
Async XLA Ops:
  6.5 18.3 %copy-start = (bf16[1,128,3072]{2,1,0:T(8,128)(2,1)S(1)}, bf16[1,128,3072]{2,1,0:T(8,128)(2,1)}, u32[]{:S(2)}) copy-start(bf16[1,128,3072]{2,1,0:T(8,128)(2,1)} %param.7) | copy-start | bytes 2359300
  6.5 55.1 %all-gather.9.cloned.1.call-start = ((), (), s32[]{:S(2)}) async-start(), calls=%async_computation.6 | async-start | bytes 2949120 | tf_op jit(solution)/shard_map/all_gather | solution.py:69
  7.3 118.2 %all-gather.5.cloned.1.call-start = ((), (), s32[]{:S(2)}) async-start(), calls=%async_computation.4 | async-start | bytes 3932160 | tf_op jit(solution)/shard_map/all_gather | solution.py:38
  24.8 164.3 %all-gather.7.cloned.1.call-start = ((), (), s32[]{:S(2)}) async-start(), calls=%async_computation.5 | async-start | bytes 3932160 | tf_op jit(solution)/shard_map/all_gather | solution.py:39
  25.3 36.4 %copy-start.1 = (bf16[1,128,3072]{2,1,0:T(8,128)(2,1)S(1)}, bf16[1,128,3072]{2,1,0:T(8,128)(2,1)}, u32[]{:S(2)}) copy-start(bf16[1,128,3072]{2,1,0:T(8,128)(2,1)} %param.5) | copy-start | bytes 2359300
  39.0 254.6 %all-gather.11.cloned.1.call-start = ((), (), s32[]{:S(2)}) async-start(), calls=%async_computation.7 | async-start | bytes 21233664 | tf_op jit(solution)/shard_map/all_gather | solution.py:72
  62.8 14.4 %all-to-all-start.1 = ((bf16[128,2,1536]{0,2,1:T(8,128)(2,1)}), bf16[128,2,1536]{0,2,1:T(8,128)(2,1)S(1)}, u32[]{:S(2)}, u32[]{:S(2)}) async-start(bf16[128,2,1536]{0,2,1:T(8,128)(2,1)} %bitcast.5), calls=%async_computation.1 | async-start | bytes 1572864 | tf_op jit(solution)/shard_map/all_to_all | solution.py:16
  208.6 1.7 copy-start.5
  210.4 1.2 copy-start.4
  211.6 1.4 copy-start.3
  212.9 1.2 copy-start.2
Sparse Core Ops, SparseCore 0:
  8.9 52.6 all-gather.8
  63.2 62.1 all-gather.4
  127.0 62.0 all-gather.6
  190.9 102.6 all-gather.10
where the time goes:
time: 311 us; the launch traced here: 310 us
  waiting for transfers between devices  190 us (61%)
  blocking collectives  44 us (14%)
  local copies, waits for them, and re-layouts  32.5 us (10%)
  matrix products  21.1 us (7%)
  between operations  14.1 us (5%)
  other arithmetic  4.22 us (1%)
  starting transfers between devices  3.66 us (1%)
    all_gather x1, waiting for transfers between devices, shards(): lax.all_gather(wide_weight, ('seq', 'bucket'), axis=0, tiled=True)  58.3 us
    all_gather x1, waiting for transfers between devices, shards(): value_rows = lax.all_gather(local_v, 'tensor', axis=0, tiled=True)  57.6 us
    all_gather x1, waiting for transfers between devices, shards(): key_rows = lax.all_gather(local_k, 'tensor', axis=0, tiled=True)  41 us
    all_gather x1, waiting for transfers between devices, shards(): wide_weight = lax.all_gather(out_weight, 'tensor', axis=1, tiled=True)  22.6 us
    all_to_all x1, blocking collectives, shards(): lax.all_to_all(mixed, 'seq', split_axis=0, concat_axis=1, tiled=True)  16.7 us
    all_to_all x1, blocking collectives, shards(): lax.all_to_all(keys[0], 'seq', split_axis=1, concat_axis=0, tiled=True)  14.8 us
    slice x5, local copies, waits for them, and re-layouts, shards(): value_rows[offset * row_count:(offset + 1) * row_count]  13.3 us
    all_to_all x1, blocking collectives, shards(): lax.all_to_all(values[0], 'seq', split_axis=1, concat_axis=0, tiled=True)  12.5 us
  transfers between devices with their start and end apart: 5, of which 5 were waited for; matrix products, arithmetic and copies ran while one was open for 15% of the time, Pallas kernels for 0%

commit v1 on v0

--- a/solution.py
+++ b/solution.py
@@ -35,7 +35,14 @@
     )
     carried = initial
     first_row = jnp.int32(0)
-    key_rows = lax.all_gather(local_k, "tensor", axis=0, tiled=True)
+    ring = [local_k]
+    for hop in range(3):
+        ring.append(lax.ppermute(ring[-1], "tensor", [(dev, (dev + 1) % 4) for dev in range(4)]))
+    key_rows = jnp.roll(
+        jnp.concatenate(ring[::-1], axis=0),
+        (lax.axis_index("tensor") + 1) * ring[0].shape[0],
+        axis=0,
+    )
     value_rows = lax.all_gather(local_v, "tensor", axis=0, tiled=True)
     for offset in range(key_rows.shape[0] // row_count):
         row_peak, row_sum, accumulated = carried

time: 311 us -> 285 us (0.916)
  waiting for transfers between devices: 190 us -> 138 us
  starting transfers between devices: 3.66 us -> 16.6 us
  local copies, waits for them, and re-layouts: 32.5 us -> 39.4 us
  blocking collectives: 44 us -> 50.4 us
    ppermute x0 -> x3, waiting for transfers between devices: none -> 70.4 us  [shards(): lax.ppermute(ring[-1], 'tensor', [(dev, (dev + 1) % 4) for dev in range(4)])]
    all_gather x1, waiting for transfers between devices: 57.6 us -> 0.02 us  [shards(): value_rows = lax.all_gather(local_v, 'tensor', axis=0, tiled=True)]
    all_gather x1, waiting for transfers between devices: 58.3 us -> 10.4 us  [shards(): lax.all_gather(wide_weight, ('seq', 'bucket'), axis=0, tiled=True)]
    all_gather x1 -> x0, waiting for transfers between devices: 41 us -> none  [shards(): key_rows = lax.all_gather(local_k, 'tensor', axis=0, tiled=True)]
    all_gather x1, waiting for transfers between devices: 22.6 us -> 36.6 us  [shards(): wide_weight = lax.all_gather(out_weight, 'tensor', axis=1, tiled=True)]
    ppermute x0 -> x3, starting transfers between devices: none -> 12.9 us  [shards(): lax.ppermute(ring[-1], 'tensor', [(dev, (dev + 1) % 4) for dev in range(4)])]
    all_to_all x1, waiting for transfers between devices: 10.2 us -> 19.3 us  [shards(): lax.all_to_all(queries[0], 'seq', split_axis=1, concat_axis=0, tiled=True)]
    unnamed x15 -> x34, local copies, waits for them, and re-layouts: 3.05 us -> 10.3 us
  transfers between devices with their start and end apart: 5 -> 7, of which waited for: 5 -> 5; matrix products, arithmetic and copies ran while one was open for 15% -> 18% of each run, Pallas kernels for 0% -> 0%
where the time goes in v1:
time: 285 us
  waiting for transfers between devices  138 us (48%)
  blocking collectives  50.4 us (18%)
  local copies, waits for them, and re-layouts  39.4 us (14%)
  matrix products  22.4 us (8%)
  starting transfers between devices  16.6 us (6%)
  between operations  14.1 us (5%)
  other arithmetic  4.3 us (2%)
    ppermute x3, waiting for transfers between devices, shards(): lax.ppermute(ring[-1], 'tensor', [(dev, (dev + 1) % 4) for dev in range(4)])  70.4 us
    all_gather x1, waiting for transfers between devices, shards(): wide_weight = lax.all_gather(out_weight, 'tensor', axis=1, tiled=True)  36.6 us
    all_to_all x1, blocking collectives, shards(): lax.all_to_all(mixed, 'seq', split_axis=0, concat_axis=1, tiled=True)  22.1 us
    all_to_all x1, waiting for transfers between devices, shards(): lax.all_to_all(queries[0], 'seq', split_axis=1, concat_axis=0, tiled=True)  19.3 us
    all_to_all x1, blocking collectives, shards(): lax.all_to_all(values[0], 'seq', split_axis=1, concat_axis=0, tiled=True)  14.9 us
    all_to_all x1, blocking collectives, shards(): lax.all_to_all(keys[0], 'seq', split_axis=1, concat_axis=0, tiled=True)  13.3 us
    ppermute x3, starting transfers between devices, shards(): lax.ppermute(ring[-1], 'tensor', [(dev, (dev + 1) % 4) for dev in range(4)])  12.9 us
    slice x5, local copies, waits for them, and re-layouts, shards(): value_rows[offset * row_count:(offset + 1) * row_count]  12.9 us
  transfers between devices with their start and end apart: 7, of which 5 were waited for; matrix products, arithmetic and copies ran while one was open for 18% of the time, Pallas kernels for 0%

profile of v1, /device:TPU:0, one launch (start us, length us, event | category | flops | bytes accessed | tf_op | source)
XLA Modules:
  0.0 284.7 jit_solution(3637348218246623056)
XLA Ops:
  6.5 0.7 all-gather.6.cloned.1.call-update
  7.3 0.0 all-gather.4.cloned.1.call-start
  7.3 1.5 copy.75
  8.8 14.9 %all_to_all.70 = bf16[128,2,1536]{0,2,1:T(8,128)(2,1)S(1)} all-to-all(bf16[128,2,1536]{0,2,1:T(8,128)(2,1)S(1)} %bitcast.128), channel_id=1, replica_groups=mesh['seq'=2,'tensor'=4,'bucket'=4] {'seq'}, dimensions={1} | all-to-all | bytes 1572864 | tf_op jit(solution)/shard_map/all_to_all | solution.py:18
  23.8 1.2 copy.76
  25.0 0.0 all-gather.8.cloned.1.call-start
  25.0 36.6 %all-gather.6.cloned.1.call-done = bf16[384,3072]{1,0:T(8,128)(2,1)} async-done(((bf16[384,768]{1,0:T(8,128)(2,1)}), bf16[384,3072]{1,0:T(8,128)(2,1)}) %all-gather.6.cloned.1.call-update) | async-done | bytes 2359312 | tf_op jit(solution)/shard_map/all_gather | solution.py:76
  61.7 0.4 copy.68
  62.1 13.3 %all_to_all.71 = bf16[128,2,1536]{0,2,1:T(8,128)(2,1)S(1)} all-to-all(bf16[128,2,1536]{0,2,1:T(8,128)(2,1)S(1)} %bitcast.129), channel_id=1, replica_groups=mesh['seq'=2,'tensor'=4,'bucket'=4] {'seq'}, dimensions={1} | all-to-all | bytes 1572864 | tf_op jit(solution)/shard_map/all_to_all | solution.py:17
  75.4 0.3 copy.69
  75.7 0.1 collective-permute-start
  75.7 38.4 %collective-permute-done = bf16[256,1536]{1,0:T(8,128)(2,1)S(1)} collective-permute-done((bf16[256,1536]{1,0:T(8,128)(2,1)S(1)}, bf16[256,1536]{1,0:T(8,128)(2,1)S(1)}, u32[]{:S(2)}, u32[]{:S(2)}) %collective-permute-start) | collective-permute-done | bytes 786464 | tf_op jit(solution)/shard_map/ppermute | solution.py:40
  114.1 12.9 %collective-permute-start.1 = (bf16[256,1536]{1,0:T(8,128)(2,1)S(1)}, bf16[256,1536]{1,0:T(8,128)(2,1)S(1)}, u32[]{:S(2)}, u32[]{:S(2)}) collective-permute-start(bf16[256,1536]{1,0:T(8,128)(2,1)S(1)} %collective-permute-done), channel_id=1, source_target_pairs={{0,4},{4,8},{8,12},{12,0},{1,5},{5,9},{9,13},{13,1},{2,6},{6,10},{... | collective-permute-start | bytes 2359304 | tf_op jit(solution)/shard_map/ppermute | solution.py:40
  127.0 32.0 %collective-permute-done.1 = bf16[256,1536]{1,0:T(8,128)(2,1)S(1)} collective-permute-done((bf16[256,1536]{1,0:T(8,128)(2,1)S(1)}, bf16[256,1536]{1,0:T(8,128)(2,1)S(1)}, u32[]{:S(2)}, u32[]{:S(2)}) %collective-permute-start.1) | collective-permute-done | bytes 786464 | tf_op jit(solution)/shard_map/ppermute | solution.py:40
  159.0 2.3 copy.71
  161.3 3.6 %all-to-all-start.1 = ((bf16[128,2,1536]{0,2,1:T(8,128)(2,1)}), bf16[128,2,1536]{0,2,1:T(8,128)(2,1)S(1)}, u32[]{:S(2)}, u32[]{:S(2)}) async-start(bf16[128,2,1536]{0,2,1:T(8,128)(2,1)} %bitcast.125), calls=%async_computation.1 | async-start | bytes 1572864 | tf_op jit(solution)/shard_map/all_to_all | solution.py:16
  165.7 19.3 %all-to-all-done.1 = bf16[128,2,1536]{0,2,1:T(8,128)(2,1)S(1)} async-done(((bf16[128,2,1536]{0,2,1:T(8,128)(2,1)}), bf16[128,2,1536]{0,2,1:T(8,128)(2,1)S(1)}, u32[]{:S(2)}, u32[]{:S(2)}) %all-to-all-start.1) | async-done | bytes 786464 | tf_op jit(solution)/shard_map/all_to_all | solution.py:16
  185.0 7.2 %copy.72 = bf16[2,128,1536]{1,0,2:T(2,128)(2,1)} copy(bf16[2,128,1536]{1,2,0:T(8,128)(2,1)S(1)} %bitcast.124) | data formatting | bytes 1572864 | tf_op jit(solution)/shard_map/all_to_all | solution.py:16
  192.3 2.6 reshape.424
  194.9 1.2 constant_dynamic-update-slice_fusion.7
  196.1 0.1 constant_dynamic-update-slice_fusion.6
  196.1 0.1 constant_dynamic-update-slice_fusion.5
  196.2 0.1 constant_dynamic-update-slice_fusion.4
  196.3 1.2 constant_dynamic-update-slice_fusion.3
  197.5 0.1 constant_dynamic-update-slice_fusion.2
  197.5 0.1 constant_dynamic-update-slice_fusion.1
  197.6 0.1 constant_dynamic-update-slice_fusion
  197.6 1.1 constant_dynamic-slice_fusion.2
  198.8 1.2 copy.86
  199.9 0.3 copy.80
  200.2 0.3 copy.70
  200.5 1.4 copy.92
  201.9 1.9 bitcast_reduce_fusion.1
  203.9 0.9 bitcast_reduce_fusion.2
  204.7 0.9 bitcast_reduce_fusion.3
  205.6 0.8 bitcast_reduce_fusion
  206.5 0.9 fusion.9
  207.4 0.5 copy-done
  207.8 1.0 copy-done.4
  208.9 0.9 fusion.11
  209.7 0.9 fusion.13
  210.6 0.3 copy-done.6
  210.9 0.9 fusion.15
  211.9 0.0 all-gather.4.cloned.1.call-done
  211.9 3.6 %fusion.88 = (bf16[256,1536]{1,0:T(8,128)(2,1)}, bf16[256,1536]{1,0:T(8,128)(2,1)}, bf16[256,1536]{1,0:T(8,128)(2,1)}, bf16[256,1536]{1,0:T(8,128)(2,1)}) fusion(bf16[1024,1536]{1,0:T(8,128)(2,1)} %all-gather.4.cloned.1.call-done), kind=kLoop, calls=%fused_computation.167 | loop fusion | bytes 6291456 | tf_op jit(solution)/shard_map/slice | solution.py:52
  215.4 2.4 copy.83
  217.9 2.3 copy.89
  220.2 2.3 copy.95
  222.5 2.3 copy.77
  224.8 2.4 fusion.21
  227.3 1.4 fusion.19
  228.7 0.5 copy-done.7
  229.2 0.2 copy-done.10
  229.4 1.1 fusion.17
  230.6 0.7 copy-done.1
  231.3 0.2 copy-done.9
  231.5 3.0 %fusion.25 = bf16[256,12,128]{2,0,1:T(8,128)(2,1)S(1)} fusion(f32[12,256,128]{2,1,0:T(8,128)S(1)} %fusion.17, f32[12,256,128]{2,1,0:T(8,128)S(1)} %fusion.19, f32[12,256,128]{2,1,0:T(8,128)S(1)} %fusion.21, f32[256,12]{0,1:T(8,128)S(1)} %get-tuple-element.5, f32[256,12]{0,1:T(8,128)S(1)} %get-tuple-element.8, f32[256,12]{0,1:T(8,128)S(1)} %get-tuple-element.7, ...), kind=kOutput, calls=%fused_computation.35 | convolution fusion | flops 208797696 | bytes 9511168 | tf_op jit(solution)/shard_map/qhk,khd->qhd/dot_general | solution.py:63
  234.5 0.3 copy.98
  234.8 0.2 reshape.432
  235.0 0.8 select_convert_fusion
  235.8 0.1 copy.99
  235.9 22.1 %all_to_all.72 = bf16[2,128,1536]{1,2,0:T(8,128)(2,1)S(1)} all-to-all(bf16[2,128,1536]{1,2,0:T(8,128)(2,1)S(1)} %copy.99), channel_id=1, replica_groups=mesh['seq'=2,'tensor'=4,'bucket'=4] {'seq'}, dimensions={0} | all-to-all | bytes 1572864 | tf_op jit(solution)/shard_map/all_to_all | solution.py:75
  257.9 10.4 %all-gather.8.cloned.1.call-done = bf16[3072,3072]{1,0:T(8,128)(2,1)} async-done(((bf16[384,3072]{1,0:T(8,128)(2,1)}), bf16[3072,3072]{1,0:T(8,128)(2,1)}) %all-gather.8.cloned.1.call-update) | async-done | bytes 18874384 | tf_op jit(solution)/shard_map/all_gather | solution.py:79
  268.3 9.9 %fusion = bf16[1,128,3072]{2,1,0:T(8,128)(2,1)} fusion(bf16[128,3072]{0,1:T(8,128)(2,1)S(1)} %bitcast.118, bf16[3072,3072]{1,0:T(8,128)(2,1)} %all-gather.8.cloned.1.call-done), kind=kOutput, calls=%fused_computation.1 | convolution fusion | flops 2416312320 | bytes 20447232 | tf_op jit(solution)/shard_map/dot_general | solution.py:77
  (27 shorter events, 0.2 us)
Async XLA Ops:
  6.5 55.1 %all-gather.6.cloned.1.call-start = ((), (), s32[]{:S(2)}) async-start(), calls=%async_computation.5 | async-start | bytes 2949120 | tf_op jit(solution)/shard_map/all_gather | solution.py:76
  7.3 204.6 %all-gather.4.cloned.1.call-start = ((), (), s32[]{:S(2)}) async-start(), calls=%async_computation.4 | async-start | bytes 3932160 | tf_op jit(solution)/shard_map/all_gather | solution.py:46
  8.8 52.9 %copy-start.8 = (bf16[1,128,3072]{2,1,0:T(8,128)(2,1)S(1)}, bf16[1,128,3072]{2,1,0:T(8,128)(2,1)}, u32[]{:S(2)}) copy-start(bf16[1,128,3072]{2,1,0:T(8,128)(2,1)} %param.6) | copy-start | bytes 2359300
  25.0 243.3 %all-gather.8.cloned.1.call-start = ((), (), s32[]{:S(2)}) async-start(), calls=%async_computation.6 | async-start | bytes 21233664 | tf_op jit(solution)/shard_map/all_gather | solution.py:79
  75.7 38.5 %collective-permute-start = (bf16[256,1536]{1,0:T(8,128)(2,1)S(1)}, bf16[256,1536]{1,0:T(8,128)(2,1)S(1)}, u32[]{:S(2)}, u32[]{:S(2)}) collective-permute-start(bf16[256,1536]{1,0:T(8,128)(2,1)S(1)} %bitcast.115), channel_id=1, source_target_pairs={{0,4},{4,8},{8,12},{12,0},{1,5},{5,9},{9,13},{13,1},{2,6},{6,10},{... | collective-permute-start | bytes 2359304 | tf_op jit(solution)/shard_map/ppermute | solution.py:40
  114.1 44.9 %collective-permute-start.1 = (bf16[256,1536]{1,0:T(8,128)(2,1)S(1)}, bf16[256,1536]{1,0:T(8,128)(2,1)S(1)}, u32[]{:S(2)}, u32[]{:S(2)}) collective-permute-start(bf16[256,1536]{1,0:T(8,128)(2,1)S(1)} %collective-permute-done), channel_id=1, source_target_pairs={{0,4},{4,8},{8,12},{12,0},{1,5},{5,9},{9,13},{13,1},{2,6},{6,10},{... | collective-permute-start | bytes 2359304 | tf_op jit(solution)/shard_map/ppermute | solution.py:40
  159.0 35.9 %collective-permute-start.2 = (bf16[256,1536]{1,0:T(8,128)(2,1)S(1)}, bf16[256,1536]{1,0:T(8,128)(2,1)}, u32[]{:S(2)}, u32[]{:S(2)}) collective-permute-start(bf16[256,1536]{1,0:T(8,128)(2,1)S(1)} %collective-permute-done.1), channel_id=1, source_target_pairs={{0,4},{4,8},{8,12},{12,0},{1,5},{5,9},{9,13},{13,1},{2,6},{6,10},{... | collective-permute-start | bytes 2359304 | tf_op jit(solution)/shard_map/ppermute | solution.py:40
  161.3 23.7 %all-to-all-start.1 = ((bf16[128,2,1536]{0,2,1:T(8,128)(2,1)}), bf16[128,2,1536]{0,2,1:T(8,128)(2,1)S(1)}, u32[]{:S(2)}, u32[]{:S(2)}) async-start(bf16[128,2,1536]{0,2,1:T(8,128)(2,1)} %bitcast.125), calls=%async_computation.1 | async-start | bytes 1572864 | tf_op jit(solution)/shard_map/all_to_all | solution.py:16
  203.9 5.9 %copy-start.2 = (f32[12,256,256]{2,1,0:T(8,128)}, f32[12,256,256]{2,1,0:T(8,128)S(1)}, u32[]{:S(2)}) copy-start(f32[12,256,256]{2,1,0:T(8,128)S(1)} %get-tuple-element.25) | copy-start | bytes 9437188
  204.7 4.1 %copy-start.4 = (f32[12,256,256]{2,1,0:T(8,128)}, f32[12,256,256]{2,1,0:T(8,128)S(1)}, u32[]{:S(2)}) copy-start(f32[12,256,256]{2,1,0:T(8,128)S(1)} %get-tuple-element.27) | copy-start | bytes 9437188
  205.6 2.2 copy-start
  206.5 4.5 %copy-start.6 = (f32[12,256,256]{2,1,0:T(8,128)}, f32[12,256,256]{2,1,0:T(8,128)S(1)}, u32[]{:S(2)}) copy-start(f32[12,256,256]{2,1,0:T(8,128)S(1)} %get-tuple-element.23) | copy-start | bytes 9437188
  215.4 9.3 %copy-start.5 = (f32[12,256,256]{2,1,0:T(8,128)S(1)}, f32[12,256,256]{2,1,0:T(8,128)}, u32[]{:S(2)}) copy-start(f32[12,256,256]{2,1,0:T(8,128)} %copy-done.4) | copy-start | bytes 9437188
  224.8 2.5 copy-start.3
  224.8 2.5 copy-start.11
  227.2 2.0 copy-start.7
  227.2 2.1 copy-start.10
  229.4 1.9 copy-start.1
  229.4 2.1 copy-start.9
Sparse Core Ops, SparseCore 0:
  8.9 52.6 all-gather.5
  63.2 88.9 all-gather.3
  154.1 114.1 all-gather.7
